TPU v7x, 256 devices: a whole 4x4x8 slice. The times are simulated.
256 devices in a mesh: row: 32 (over z_lo, x, core), col: 8 (over z_hi, y).
Axes of the slice: x: 4, y: 4, z: 8 (z_hi: 2, z_lo: 4; z = z_hi * 4 + z_lo), core: 2. Of those that a mesh axis runs over, the one named last changes fastest.
Arguments:
- tokens: bfloat16 [2048, 8192], P('row', 'col'), may hold values from -6 to 6
- norm_gain: bfloat16 [8192], P('col'), may hold values from 0.099609375 to 1.8984375
- gate_proj: bfloat16 [8192, 28672], P('col', 'row'), may hold values from -0.0625 to 0.0625
- up_proj: bfloat16 [8192, 28672], P('col', 'row'), may hold values from -0.0625 to 0.0625
- down_proj: bfloat16 [28672, 8192], P('row', 'col'), may hold values from -0.03125 to 0.03125
Outputs:
- mixed: bfloat16 [2048, 8192], P('row', 'col')
All inputs are finite; a program needn't handle non-finite values.
Results may differ from a plain program's by a relative error of at most 0.015.
Values may be sent and summed in bfloat16 or wider, within the bound.
A program may use at most 128 MiB of HBM per device.

v0:
```python
import jax
import jax.numpy as jnp
from jax import lax
from jax.sharding import Mesh
from jax.sharding import PartitionSpec as P

D = 8192
ROW = ("row_0", "row_1", "row_2")


floor_term = 0.25


def side_by_side(arrays, axis, dim, along):
    columns = [a.reshape(*a.shape[:along], -1) for a in arrays]
    both = jnp.concatenate(columns, axis=along)
    whole, at, outs = (lax.psum_scatter(both, axis, scatter_dimension=dim, tiled=True), 0, [])
    for a, column in zip(arrays, columns):
        slab = whole[..., at : at + column.shape[along]]
        outs.append(slab.reshape(*slab.shape[:along], *a.shape[along:]))
        at += column.shape[along]
    return tuple(outs)


def cut_along(x, dim, count):
    shape = x.shape
    tiles = x.reshape(*shape[:dim], count, shape[dim] // count, *shape[dim + 1 :])
    return jnp.moveaxis(tiles, dim, 0)


def summed_rows(x, chips, core, dim):
    sizes = (lax.axis_size(chips), lax.axis_size(core))
    tiles = cut_along(x, dim, sizes[0] * sizes[1])
    inside = tiles.shape[1:]
    tiles = tiles.reshape(*sizes, *inside).swapaxes(0, 1).reshape(-1, *inside)
    tiles = lax.psum_scatter(tiles, core, scatter_dimension=0, tiled=True)
    return lax.psum_scatter(tiles, chips, scatter_dimension=0, tiled=True)[0]


def shards(tokens, norm_gain, gate_proj, up_proj, down_proj):
    gathered = lax.all_gather(tokens, ROW, axis=0, tiled=True)
    widened = gathered.astype(jnp.float32)
    partial_squares = jnp.sum(widened * widened, axis=1)
    scaled = (widened * norm_gain.astype(jnp.float32)[None, :]).astype(jnp.bfloat16)
    gate_part = jnp.dot(scaled, gate_proj, preferred_element_type=jnp.float32)
    up_part = jnp.dot(scaled, up_proj, preferred_element_type=jnp.float32)
    gate_sum, up_sum, block_squares = tuple(
        (
            part.astype(jnp.float32)
            for part in side_by_side(
                (
                    gate_part.astype(jnp.bfloat16),
                    up_part.astype(jnp.bfloat16),
                    partial_squares.astype(jnp.bfloat16),
                ),
                "col",
                0,
                1,
            )
        )
    )
    row_scale = 1.0 / jnp.sqrt(block_squares / D + floor_term)
    gate_value = row_scale[:, None] * gate_sum
    up_value = row_scale[:, None] * up_sum
    hidden = (jax.nn.silu(gate_value) * up_value).astype(jnp.bfloat16)
    partial_out = jnp.dot(
        lax.all_gather(hidden, "col", axis=0, tiled=True),
        down_proj,
        preferred_element_type=jnp.float32,
    )
    summed = summed_rows(partial_out.astype(jnp.bfloat16), ("row_0", "row_1"), "row_2", 0).astype(
        jnp.float32
    )
    return (tokens.astype(jnp.float32) + summed).astype(jnp.bfloat16)


def solution(mesh):
    split = Mesh(
        mesh.devices.reshape(4, 4, 2, mesh.shape["col"]), ("row_0", "row_1", "row_2", "col")
    )
    return jax.shard_map(
        shards,
        mesh=split,
        in_specs=(P(ROW, "col"), P("col"), P("col", ROW), P("col", ROW), P(ROW, "col")),
        out_specs=P(ROW, "col"),
        check_vma=False,
    )
```

profile of v0, /device:TPU:8, one launch (start us, length us, event | category | flops | bytes accessed | tf_op | source)
XLA Modules:
  0.0 486.7 jit_solution(9350817173539527873)
XLA Ops:
  6.5 0.7 all-gather.3.cloned.1.call-update
  7.3 0.0 reduce-scatter.4.cloned.1.call-start
  7.3 0.7 convert_element_type.58
  8.0 66.6 %all-gather.3.cloned.1.call-done = bf16[2048,1024]{1,0:T(8,128)(2,1)} async-done(((bf16[64,1024]{1,0:T(8,128)(2,1)}), bf16[2048,1024]{1,0:T(8,128)(2,1)}) %all-gather.3.cloned.1.call-update) | async-done | bytes 4194320 | tf_op jit(solution)/shard_map/all_gather | solution.py:41
  74.6 3.2 fusion.1
  77.8 0.2 copy-done.1
  78.1 5.9 %fusion.9 = bf16[2048,896]{0,1:T(8,128)(2,1)S(1)} fusion(bf16[1024,896]{1,0:T(8,128)(2,1)} %param.8, bf16[2048,1024]{1,0:T(8,128)(2,1)S(1)} %copy-done.1, f32[1024]{0:T(1024)S(1)} %convert_element_type.58), kind=kOutput, calls=%fused_computation.9 | convolution fusion | flops 3766222848 | bytes 9703424 | tf_op jit(solution)/shard_map/dot_general | solution.py:46
  83.9 4.3 fusion.6
  88.3 3.8 pad_maximum_fusion
  92.1 0.0 all-gather.5.cloned.1.call-start
  92.2 169.8 %reduce-scatter.4.cloned.1.call-done = bf16[256,1793]{0,1:T(8,128)(2,1)} async-done(((bf16[2048,1793]{0,1:T(8,128)(2,1)}), bf16[256,1793]{0,1:T(8,128)(2,1)}) %reduce-scatter.4.cloned.1.call-update) | async-done | bytes 918032 | tf_op jit(solution)/shard_map/reduce_scatter | solution.py:17
  262.0 0.7 fusion.15
  262.7 2.2 multiply_convert_fusion
  264.9 0.0 all-gather.5.cloned.1.call-update
  264.9 0.0 reduce-scatter.6.cloned.1.call-start
  265.0 98.3 %all-gather.5.cloned.1.call-done = bf16[2048,896]{0,1:T(8,128)(2,1)} async-done(((bf16[256,896]{0,1:T(8,128)(2,1)}), bf16[2048,896]{0,1:T(8,128)(2,1)}) %all-gather.5.cloned.1.call-update) | async-done | bytes 3670032 | tf_op jit(solution)/shard_map/all_gather | solution.py:67
  363.3 6.8 %convolution_convert_fusion = bf16[2048,1024]{1,0:T(8,128)(2,1)S(1)} fusion(bf16[2048,896]{0,1:T(8,128)(2,1)} %all-gather.5.cloned.1.call-done, bf16[896,1024]{1,0:T(8,128)(2,1)S(1)} %copy-done), kind=kOutput, calls=%fused_computation.5 | convolution fusion | flops 3760193536 | bytes 9699328 | tf_op jit(solution)/shard_map/dot_general | solution.py:66
  370.1 2.4 copy.6
  372.5 0.0 reduce-scatter.6.cloned.1.call-update
  372.6 0.0 reduce-scatter.8.cloned.1.call-start
  372.6 13.6 %reduce-scatter.6.cloned.1.call-done = bf16[16,64,1024]{2,1,0:T(8,128)(2,1)} async-done(((bf16[32,64,1024]{2,1,0:T(8,128)(2,1)}), bf16[16,64,1024]{2,1,0:T(8,128)(2,1)}) %reduce-scatter.6.cloned.1.call-update) | async-done | bytes 2097168 | tf_op jit(solution)/shard_map/reduce_scatter | solution.py:36
  386.2 0.0 reduce-scatter.8.cloned.1.call-update
  386.3 92.3 %reduce-scatter.8.cloned.1.call-done = bf16[1,64,1024]{2,1,0:T(8,128)(2,1)} async-done(((bf16[16,64,1024]{2,1,0:T(8,128)(2,1)}), bf16[1,64,1024]{2,1,0:T(8,128)(2,1)}) %reduce-scatter.8.cloned.1.call-update) | async-done | bytes 131088 | tf_op jit(solution)/shard_map/reduce_scatter | solution.py:37
  478.6 1.6 fusion.12
  (10 shorter events, 0.0 us)
Async XLA Ops:
  6.5 356.8 %copy-start = (bf16[896,1024]{1,0:T(8,128)(2,1)S(1)}, bf16[896,1024]{1,0:T(8,128)(2,1)}, u32[]{:S(2)}) copy-start(bf16[896,1024]{1,0:T(8,128)(2,1)} %param.9) | copy-start | bytes 5505028
  6.5 68.1 %all-gather.3.cloned.1.call-start = ((), (), s32[]{:S(2)}) async-start(), calls=%async_computation.3 | async-start | bytes 4325376 | tf_op jit(solution)/shard_map/all_gather | solution.py:41
  7.3 254.7 %reduce-scatter.4.cloned.1.call-start = ((), (), s32[]{:S(2)}) async-start(), calls=%async_computation.4 | async-start | bytes 8294400 | tf_op jit(solution)/shard_map/reduce_scatter | solution.py:17
  74.6 3.4 copy-start.1
  78.1 5.9 %copy-start.3 = (bf16[1024,896]{1,0:T(8,128)(2,1)S(1)}, bf16[1024,896]{1,0:T(8,128)(2,1)}, u32[]{:S(2)}) copy-start(bf16[1024,896]{1,0:T(8,128)(2,1)} %param.7) | copy-start | bytes 5505028
  92.1 271.2 %all-gather.5.cloned.1.call-start = ((), (), s32[]{:S(2)}) async-start(), calls=%async_computation.5 | async-start | bytes 4128768 | tf_op jit(solution)/shard_map/all_gather | solution.py:67
  264.9 121.3 %reduce-scatter.6.cloned.1.call-start = ((), (), s32[]{:S(2)}) async-start(), calls=%async_computation.6 | async-start | bytes 6291456 | tf_op jit(solution)/shard_map/reduce_scatter | solution.py:36
  372.5 106.1 %copy-start.2 = (bf16[64,1024]{1,0:T(8,128)(2,1)S(1)}, bf16[64,1024]{1,0:T(8,128)(2,1)}, u32[]{:S(2)}) copy-start(bf16[64,1024]{1,0:T(8,128)(2,1)} %param.5) | copy-start | bytes 393220
  372.6 106.0 %reduce-scatter.8.cloned.1.call-start = ((), (), s32[]{:S(2)}) async-start(), calls=%async_computation.7 | async-start | bytes 2228224 | tf_op jit(solution)/shard_map/reduce_scatter | solution.py:37
Sparse Core Ops, SparseCore 0:
  9.2 65.3 all-gather.2
  92.2 169.6 reduce-scatter.3
  265.1 98.2 all-gather.4
  372.7 13.5 reduce-scatter.5
  388.6 89.9 reduce-scatter.7
where the time goes:
time: 487 us
  waiting for transfers between devices  441 us (91%)
  matrix products  17 us (3%)
  between operations  13.2 us (3%)
  other arithmetic  12.3 us (3%)
    reduce_scatter x1, waiting for transfers between devices, side_by_side(): lax.psum_scatter(both, axis, scatter_dimension=dim, tiled=True)  170 us
    all_gather x1, waiting for transfers between devices, shards(): lax.all_gather(hidden, 'col', axis=0, tiled=True)  98.3 us
    reduce_scatter x1, waiting for transfers between devices, summed_rows(): return lax.psum_scatter(tiles, chips, scatter_dimension=0, tiled=True)[0]  92.3 us
    all_gather x1, waiting for transfers between devices, shards(): gathered = lax.all_gather(tokens, ROW, axis=0, tiled=True)  66.6 us
    reduce_scatter x1, waiting for transfers between devices, summed_rows(): tiles = lax.psum_scatter(tiles, core, scatter_dimension=0, tiled=True)  13.6 us
  transfers between devices with their start and end apart: 5, of which 5 were waited for; matrix products, arithmetic and copies ran while one was open for 0% of the time, Pallas kernels for 0%

commit v1 on v0

v1 whole, which is shorter than its diff:
```python
import jax
import jax.numpy as jnp
from jax import lax
from jax.experimental import pallas as pl
from jax.experimental.pallas import tpu as pltpu
from jax.sharding import Mesh
from jax.sharding import PartitionSpec as P

D = 8192
EPS = 0.25
MESH = pl.DeviceIdType.MESH
ROW = ("zl", "x", "core")
COL = ("zh", "y")

K = 8
F32 = jnp.float32
BF16 = jnp.bfloat16

PLAN = {
    "a2": (0.0, 4.0),
    "a3": (3.0, 4.0),
    "mm": (6.0, 7.5),
    "p2": (13.0, 7.5),
    "zs": (21.0, 7.5),
    "hid": (30.0, 7.5),
    "cy": (38.0, 9.0),
    "cf": (44.0, 9.0),
    "dn": (48.0, 9.0),
    "d2": (52.0, 9.0),
    "d3": (57.0, 9.0),
    "d4": (61.0, 9.0),
}


def order():
    steps = list(PLAN)
    keyed = []
    for s, name in enumerate(steps):
        start, period = PLAN[name]
        for k in range(K):
            keyed.append((start + period * k, s, k, name))
    keyed.sort(key=lambda e: (e[0], -e[1], e[2]))
    done, out = {}, []
    for _, s, k, name in keyed:
        out.append((name, k))
    for i, (name, k) in enumerate(out):
        s = steps.index(name)
        assert s == 0 or done.get((steps[s - 1], k), i) < i
        done[(name, k)] = i
    return out


def body(
    tok, gain, gate, up, down, out,
    wgu, wd, sq, xg, part, r1, r2, zs, zr, hg, oacc, d1s, d1r, d2s, d2r, o3, d3s, d3r,
    wsem, sqS, sqR, aS, aR, bS, bR, cS, cR, dS, dR,
):
    zl, x, core, zh, y = [lax.axis_index(n) for n in ("zl", "x", "core", "zh", "y")]
    F = gate.shape[1]
    R = tok.shape[0] // K
    PR, ZR = 8 * R, 4 * R
    C = 32 * R
    col = zh * 4 + y

    def add(v, d, n):
        return lax.rem(v + d, n)

    yp, ym, y2 = add(y, 1, 4), add(y, 3, 4), add(y, 2, 4)

    w_copies = [
        pltpu.make_async_copy(gate, wgu.at[:, pl.ds(0, F)], wsem.at[0]),
        pltpu.make_async_copy(up, wgu.at[:, pl.ds(F, F)], wsem.at[1]),
        pltpu.make_async_copy(down, wd, wsem.at[2]),
    ]
    for c in w_copies:
        c.start()

    def colpeer(d):
        t = add(col, d, 8)
        return {"zh": t // 4, "y": lax.rem(t, 4)}

    peers = [colpeer(d) for d in range(1, 8)]
    peers += [{"zl": add(zl, d, 4)} for d in (1, 2, 3)]
    peers += [{"x": add(x, d, 4)} for d in (1, 2, 3)]
    peers += [{"core": 1 - core}]
    barrier = pltpu.get_barrier_semaphore()
    for p in peers:
        pl.semaphore_signal(barrier, inc=1, device_id=p, device_id_type=MESH)

    pending = []

    def send(src, dst, ss, rs, dev):
        c = pltpu.make_async_remote_copy(
            src_ref=src, dst_ref=dst, send_sem=ss, recv_sem=rs, device_id=dev, device_id_type=MESH
        )
        c.start()
        pending.append(c)

    def recv(dst, ss, rs, dev):
        pltpu.make_async_remote_copy(
            src_ref=dst, dst_ref=dst, send_sem=ss, recv_sem=rs, device_id=dev, device_id_type=MESH
        ).wait_recv()

    tw = tok[...].astype(F32)
    acc = jnp.zeros((tok.shape[0], 128), F32)
    for g in range(tok.shape[1] // 128):
        v = tw[:, g * 128 : (g + 1) * 128]
        acc = acc + v * v
    acc = jnp.concatenate([acc, jnp.zeros((128 - tok.shape[0], 128), F32)], axis=0)
    sq[col] = jnp.broadcast_to(jnp.sum(acc.T, axis=0, keepdims=True), (8, 128))
    pl.semaphore_wait(barrier, len(peers))
    for d in range(1, 8):
        send(sq.at[col], sq.at[col], sqS.at[d], sqR.at[d], colpeer(d))
    for d in range(1, 8):
        t = add(col, 8 - d, 8)
        recv(sq.at[t], sqS.at[d], sqR.at[d], colpeer(d))
    total = sq[0]
    for c in range(1, 8):
        total = total + sq[c]
    scale = 1.0 / jnp.sqrt(total / D + EPS)
    scale = jnp.broadcast_to(scale[0:1, :], (128, 128)).T[: tok.shape[0], :]
    for g in range(tok.shape[1] // 128):
        cols = slice(g * 128, (g + 1) * 128)
        xn = (tok[:, cols].astype(F32) * gain[:, cols].astype(F32) * scale).astype(BF16)
        for k in range(K):
            xg[k, core, x, zl, :, cols] = xn[k * R : (k + 1) * R]
    for k in range(K):
        mine = xg.at[k, core, x, zl]
        for d in (1, 2, 3):
            send(mine, mine, aS.at[k, d - 1], aR.at[k, d - 1], {"zl": add(zl, d, 4)})

    def a2(k):
        for d in (1, 2, 3):
            s = add(zl, 4 - d, 4)
            recv(xg.at[k, core, x, s], aS.at[k, d - 1], aR.at[k, d - 1], {"zl": s})
        mine = xg.at[k, core, x]
        for d in (1, 2, 3):
            send(mine, mine, aS.at[k, d + 2], aR.at[k, d + 2], {"x": add(x, d, 4)})

    def a3(k):
        for d in (1, 2, 3):
            s = add(x, 4 - d, 4)
            recv(xg.at[k, core, s], aS.at[k, d + 2], aR.at[k, d + 2], {"x": s})
        mine = xg.at[k, core]
        send(mine, mine, aS.at[k, 6], aR.at[k, 6], {"core": 1 - core})

    def mm(k):
        recv(xg.at[k, 1 - core], aS.at[k, 6], aR.at[k, 6], {"core": 1 - core})
        if k == 0:
            w_copies[0].wait()
            w_copies[1].wait()

        def tile(n, carry):
            cols = pl.ds(pl.multiple_of(n * 256, 256), 256)
            r = jnp.dot(
                xg[k].reshape(C, xg.shape[-1]), wgu[:, cols], preferred_element_type=F32
            )
            part[k, :, :, cols] = r.astype(BF16).reshape(4, PR, 256)
            return carry

        lax.fori_loop(0, 2 * F // 256, tile, 0)
        send(part.at[k, y2, :, pl.ds(0, F)], r1.at[k, 0], bS.at[k, 0], bR.at[k, 0], {"y": yp})
        send(part.at[k, y2, :, pl.ds(F, F)], r1.at[k, 1], bS.at[k, 1], bR.at[k, 1], {"y": ym})

    def p2(k):
        recv(r1.at[k, 0], bS.at[k, 0], bR.at[k, 0], {"y": ym})
        a = part[k, yp, :, :F].astype(F32) + r1[k, 0].astype(F32)
        part[k, yp, :, :F] = a.astype(BF16)
        send(part.at[k, yp], r2.at[k, 0], bS.at[k, 2], bR.at[k, 2], {"y": yp})
        recv(r1.at[k, 1], bS.at[k, 1], bR.at[k, 1], {"y": yp})
        a = part[k, ym, :, F:].astype(F32) + r1[k, 1].astype(F32)
        part[k, ym, :, F:] = a.astype(BF16)
        send(part.at[k, ym], r2.at[k, 1], bS.at[k, 3], bR.at[k, 3], {"y": ym})

    def ysum(k, z, cols):
        rows = pl.ds(pl.multiple_of(z * ZR, ZR), ZR)
        s = part[k, y, rows, cols].astype(F32)
        return s + r2[k, 0, rows, cols].astype(F32) + r2[k, 1, rows, cols].astype(F32)

    def zsend(k):
        recv(r2.at[k, 0], bS.at[k, 2], bR.at[k, 2], {"y": ym})
        recv(r2.at[k, 1], bS.at[k, 3], bR.at[k, 3], {"y": yp})
        for cols in (slice(0, F), slice(F, 2 * F)):
            zs[k, :, cols] = ysum(k, 1 - zh, cols).astype(BF16)
        send(zs.at[k], zr.at[k], bS.at[k, 4], bR.at[k, 4], {"zh": 1 - zh})

    def hid(k):
        recv(zr.at[k], bS.at[k, 4], bR.at[k, 4], {"zh": 1 - zh})
        g = ysum(k, zh, slice(0, F)) + zr[k, :, :F].astype(F32)
        u = ysum(k, zh, slice(F, 2 * F)) + zr[k, :, F:].astype(F32)
        hg[k, y, zh] = (jax.nn.silu(g) * u).astype(BF16)
        mine = hg.at[k, y, zh]
        send(mine, mine, cS.at[k, 0], cR.at[k, 0], {"zh": 1 - zh})

    def cy(k):
        recv(hg.at[k, y, 1 - zh], cS.at[k, 0], cR.at[k, 0], {"zh": 1 - zh})
        mine = hg.at[k, y]
        send(mine, mine, cS.at[k, 1], cR.at[k, 1], {"y": yp})
        send(mine, mine, cS.at[k, 2], cR.at[k, 2], {"y": ym})

    def cf(k):
        recv(hg.at[k, ym], cS.at[k, 1], cR.at[k, 1], {"y": ym})
        send(hg.at[k, ym, 0], hg.at[k, ym, 0], cS.at[k, 3], cR.at[k, 3], {"y": yp})
        recv(hg.at[k, yp], cS.at[k, 2], cR.at[k, 2], {"y": yp})
        send(hg.at[k, yp, 1], hg.at[k, yp, 1], cS.at[k, 4], cR.at[k, 4], {"y": ym})

    def dn(k):
        recv(hg.at[k, y2, 0], cS.at[k, 3], cR.at[k, 3], {"y": ym})
        recv(hg.at[k, y2, 1], cS.at[k, 4], cR.at[k, 4], {"y": yp})
        if k == 0:
            w_copies[2].wait()

        def tile(n, carry):
            cols = pl.ds(pl.multiple_of(n * 256, 256), 256)
            r = jnp.dot(hg[k].reshape(C, F), wd[:, cols], preferred_element_type=F32)
            both = r.reshape(2, 4, 4 * R, 256)
            oacc[k, :, :, :, cols] = both
            return carry

        lax.fori_loop(0, wd.shape[1] // 256, tile, 0)
        d1s[k] = oacc[k, 1 - core].astype(BF16)
        send(d1s.at[k], d1r.at[k], dS.at[k, 0], dR.at[k, 0], {"core": 1 - core})

    def d2(k):
        recv(d1r.at[k], dS.at[k, 0], dR.at[k, 0], {"core": 1 - core})
        for j in range(4):
            s = oacc[k, core, j] + d1r[k, j].astype(F32)
            oacc[k, core, j] = s
            d2s[k, j] = s.astype(BF16)
        for d in (1, 2, 3):
            t = add(x, d, 4)
            send(d2s.at[k, t], d2r.at[k, d - 1], dS.at[k, d], dR.at[k, d], {"x": t})

    def d3(k):
        s = oacc[k, core, x]
        for d in (1, 2, 3):
            recv(d2r.at[k, d - 1], dS.at[k, d], dR.at[k, d], {"x": add(x, d, 4)})
            s = s + d2r[k, d - 1].astype(F32)
        s = s.reshape(4, R, s.shape[-1])
        o3[k] = s
        d3s[k] = s.astype(BF16)
        for d in (1, 2, 3):
            t = add(zl, d, 4)
            send(d3s.at[k, t], d3r.at[k, d - 1], dS.at[k, d + 3], dR.at[k, d + 3], {"zl": t})

    def d4(k):
        s = tok[k * R : (k + 1) * R, :].astype(F32) + o3[k, zl]
        for d in (1, 2, 3):
            recv(d3r.at[k, d - 1], dS.at[k, d + 3], dR.at[k, d + 3], {"zl": add(zl, d, 4)})
            s = s + d3r[k, d - 1].astype(F32)
        out[k * R : (k + 1) * R, :] = s.astype(BF16)

    ops = dict(a2=a2, a3=a3, mm=mm, p2=p2, zs=zsend, hid=hid, cy=cy, cf=cf, dn=dn, d2=d2, d3=d3, d4=d4)
    for name, k in order():
        ops[name](k)
    for c in pending:
        c.wait_send()


def shards(tokens, norm_gain, gate_proj, up_proj, down_proj):
    T, DB = tokens.shape
    F = gate_proj.shape[1]
    R = T // K
    PR, ZR = 8 * R, 4 * R
    vmem = pl.BlockSpec(memory_space=pltpu.VMEM)
    hbm = pl.BlockSpec(memory_space=pl.ANY)
    dma = pltpu.SemaphoreType.DMA
    return pl.pallas_call(
        body,
        out_shape=jax.ShapeDtypeStruct((T, DB), BF16),
        in_specs=[vmem, vmem, hbm, hbm, hbm],
        out_specs=vmem,
        scratch_shapes=[
            pltpu.VMEM((DB, 2 * F), BF16),
            pltpu.VMEM((F, DB), BF16),
            pltpu.VMEM((8, 8, 128), F32),
            pltpu.VMEM((K, 2, 4, 4, R, DB), BF16),
            pltpu.VMEM((K, 4, PR, 2 * F), BF16),
            pltpu.VMEM((K, 2, PR, F), BF16),
            pltpu.VMEM((K, 2, PR, 2 * F), BF16),
            pltpu.VMEM((K, ZR, 2 * F), BF16),
            pltpu.VMEM((K, ZR, 2 * F), BF16),
            pltpu.VMEM((K, 4, 2, ZR, F), BF16),
            pltpu.VMEM((K, 2, 4, 4 * R, DB), F32),
            pltpu.VMEM((K, 4, 4 * R, DB), BF16),
            pltpu.VMEM((K, 4, 4 * R, DB), BF16),
            pltpu.VMEM((K, 4, 4 * R, DB), BF16),
            pltpu.VMEM((K, 3, 4 * R, DB), BF16),
            pltpu.VMEM((K, 4, R, DB), F32),
            pltpu.VMEM((K, 4, R, DB), BF16),
            pltpu.VMEM((K, 3, R, DB), BF16),
            dma((3,)),
            dma((8,)),
            dma((8,)),
            dma((K, 7)),
            dma((K, 7)),
            dma((K, 5)),
            dma((K, 5)),
            dma((K, 5)),
            dma((K, 5)),
            dma((K, 7)),
            dma((K, 7)),
        ],
        compiler_params=pltpu.CompilerParams(
            collective_id=0, has_side_effects=True, vmem_limit_bytes=60 * 2**20
        ),
        name="ffn",
    )(tokens, norm_gain.reshape(1, -1), gate_proj, up_proj, down_proj)


def solution(mesh):
    split = Mesh(mesh.devices.reshape(4, 4, 2, 2, 4), ROW + COL)
    return jax.shard_map(
        shards,
        mesh=split,
        in_specs=(P(ROW, COL), P(COL), P(COL, ROW), P(COL, ROW), P(ROW, COL)),
        out_specs=P(ROW, COL),
        check_vma=False,
    )
```

time: 487 us -> 181 us (0.37)
  the two profiles are of different devices: /device:TPU:8 before, /device:TPU:128 now
where the time goes in v1:
time: 181 us
  Pallas kernels  178 us (98%)
  local copies, waits for them, and re-layouts  2.85 us (2%)
    pallas_call x1, Pallas kernels, shards(): pl.pallas_call(body, out_shape=jax.ShapeDtypeStruct((T, DB), BF16), in_sp...  178 us

profile of v1, /device:TPU:128, one launch (start us, length us, event | category | flops | bytes accessed | tf_op | source)
XLA Modules:
  0.0 181.0 jit_solution(13008261836174087858)
XLA Ops:
  0.0 1.3 reshape.3.gain
  1.3 178.2 %ffn.1 = bf16[64,1024]{1,0:T(8,128)(2,1)} custom-call(bf16[64,1024]{1,0:T(8,128)(2,1)} %tok.1, bf16[1,1024]{1,0:T(2,128)(2,1)} %reshape.3.gain, bf16[1024,896]{1,0:T(8,128)(2,1)} %gate.1, bf16[1024,896]{1,0:T(8,128)(2,1)} %up.1, bf16[896,1024]{1,0:T(8,128)(2,1)} %down.1), custom_call_target="tpu_custom_call" | custom-call | tf_op jit(solution)/shard_map/ffn/pallas_call | solution.py:268
  179.5 1.6 copy.7

commit v2 on v1

v2 whole, which is shorter than its diff:
```python
import jax
import jax.numpy as jnp
from jax import lax
from jax.experimental import pallas as pl
from jax.experimental.pallas import tpu as pltpu
from jax.sharding import Mesh
from jax.sharding import PartitionSpec as P

D = 8192
EPS = 0.25
MESH = pl.DeviceIdType.MESH
ROW = ("zl", "x", "core")
COL = ("zh", "y")

K = 8
F32 = jnp.float32
BF16 = jnp.bfloat16

STEPS = ("a2", "a3", "mm", "p2", "zs", "hid", "cy", "cf", "dn", "d2", "d3", "d4", "s1", "s2", "s3", "s4")
ORDER = (
    0, 1, 4, 16, 2, 32, 33, 17, 34, 48, 3, 192, 6, 20, 49, 18, 35, 208, 50, 37,
    41, 64, 7, 5, 19, 224, 40, 65, 36, 53, 240, 80, 57, 23, 21, 66, 43, 38, 52, 69,
    81, 51, 42, 82, 56, 54, 59, 67, 73, 68, 97, 39, 85, 58, 72, 83, 22, 44, 113, 84,
    55, 75, 45, 70, 60, 71, 129, 61, 96, 101, 74, 98, 47, 100, 89, 91, 112, 88, 76, 99,
    87, 90, 86, 46, 63, 77, 128, 62, 117, 114, 116, 103, 79, 115, 78, 133, 102, 130, 105, 104,
    144, 106, 132, 93, 119, 146, 92, 95, 131, 121, 118, 94, 145, 107, 120, 108, 135, 134, 162, 122,
    109, 147, 136, 123, 110, 137, 148, 124, 125, 111, 138, 139, 149, 126, 140, 127, 141, 150, 163, 164,
    160, 142, 143, 151, 179, 165, 161, 166, 176, 167, 177, 181, 182, 180, 178, 183,
)


def own_half(j):
    return (j % 2 == 0) == (j // 2 < K // 2)


def body(
    tok_hbm, gain_hbm, gate, up, down, out,
    tok, gain, wgu, wd, sq, sg, sc, xg, part, r1, r2, zs, zr, hg, oacc, d1s, d1r, d2s, d2r, o3, d3s, d3r,
    wsem, sqS, sqR, eS, eR, aS, aR, bS, bR, cS, cR, dS, dR,
):
    zl, x, core, zh, y = [lax.axis_index(n) for n in ("zl", "x", "core", "zh", "y")]
    F = gate.shape[1]
    R = tok.shape[0] // K
    PR, ZR, C = 4 * R, 2 * R, 16 * R
    col = zh * 4 + y

    def add(v, d, n):
        return lax.rem(v + d, n)

    yp, ym, y2 = add(y, 1, 4), add(y, 3, 4), add(y, 2, 4)

    t_copy = pltpu.make_async_copy(tok_hbm, tok, wsem.at[3])
    t_copy.start()
    g_copy = pltpu.make_async_copy(gain_hbm, gain, wsem.at[4])
    g_copy.start()
    w_copies = [
        pltpu.make_async_copy(gate, wgu.at[:, pl.ds(0, F)], wsem.at[0]),
        pltpu.make_async_copy(up, wgu.at[:, pl.ds(F, F)], wsem.at[1]),
        pltpu.make_async_copy(down, wd, wsem.at[2]),
    ]
    for c in w_copies:
        c.start()

    def colpeer(d):
        t = add(col, d, 8)
        return {"zh": t // 4, "y": lax.rem(t, 4)}

    peers = [colpeer(d) for d in range(1, 8)]
    peers += [{"zl": add(zl, d, 4)} for d in (1, 2, 3)]
    peers += [{"x": add(x, d, 4)} for d in (1, 2, 3)]
    peers += [{"core": 1 - core}]
    barrier = pltpu.get_barrier_semaphore()
    for p in peers:
        pl.semaphore_signal(barrier, inc=1, device_id=p, device_id_type=MESH)

    pending = []

    def send(src, dst, ss, rs, dev):
        c = pltpu.make_async_remote_copy(
            src_ref=src, dst_ref=dst, send_sem=ss, recv_sem=rs, device_id=dev, device_id_type=MESH
        )
        c.start()
        pending.append(c)

    def recv(dst, ss, rs, dev):
        pltpu.make_async_remote_copy(
            src_ref=dst, dst_ref=dst, send_sem=ss, recv_sem=rs, device_id=dev, device_id_type=MESH
        ).wait_recv()

    t_copy.wait()
    g_copy.wait()
    gain_row = gain[...].reshape(1, -1).astype(F32)
    acc = jnp.zeros((tok.shape[0], 128), F32)
    for g in range(tok.shape[1] // 128):
        cols = slice(g * 128, (g + 1) * 128)
        v = tok[:, cols].astype(F32)
        acc = acc + v * v
        v = (v * gain_row[:, cols]).astype(BF16)
        for k in range(K):
            xg[k, core, x, zl, :, cols] = v[k * R : (k + 1) * R]
    acc = jnp.concatenate([acc, jnp.zeros((128 - tok.shape[0], 128), F32)], axis=0)
    sq[col] = jnp.broadcast_to(jnp.sum(acc.T, axis=0, keepdims=True), (8, 128))
    pl.semaphore_wait(barrier, len(peers))

    def a1(k):
        mine = xg.at[k, core, x, zl]
        for d in (1, 2, 3):
            send(mine, mine, aS.at[k, d - 1], aR.at[k, d - 1], {"zl": add(zl, d, 4)})

    a1(0)
    for d in range(1, 8):
        send(sq.at[col], sq.at[col], sqS.at[d], sqR.at[d], colpeer(d))
    for k in range(1, K):
        a1(k)

    def s1(_):
        for d in range(1, 8):
            t = add(col, 8 - d, 8)
            recv(sq.at[t], sqS.at[d], sqR.at[d], colpeer(d))
        total = sq[0]
        for c in range(1, 8):
            total = total + sq[c]
        sg[core, x, zl] = 1.0 / jnp.sqrt(total / D + EPS)
        mine = sg.at[core, x, zl]
        for d in (1, 2, 3):
            send(mine, mine, eS.at[d - 1], eR.at[d - 1], {"zl": add(zl, d, 4)})

    def s2(_):
        for d in (1, 2, 3):
            s = add(zl, 4 - d, 4)
            recv(sg.at[core, x, s], eS.at[d - 1], eR.at[d - 1], {"zl": s})
        mine = sg.at[core, x]
        for d in (1, 2, 3):
            send(mine, mine, eS.at[d + 2], eR.at[d + 2], {"x": add(x, d, 4)})

    def s3(_):
        for d in (1, 2, 3):
            s = add(x, 4 - d, 4)
            recv(sg.at[core, s], eS.at[d + 2], eR.at[d + 2], {"x": s})
        mine = sg.at[core]
        send(mine, mine, eS.at[6], eR.at[6], {"core": 1 - core})

    def s4(_):
        recv(sg.at[1 - core], eS.at[6], eR.at[6], {"core": 1 - core})
        for h in (0, 1):
            for i in (0, 1):
                v = jnp.broadcast_to(sg[h, y, 2 * zh + i][0:1, :], (128, 128)).T
                sc[h, :, i] = v[: K * R, :].reshape(K, R, 128)

    def a2(k):
        for d in (1, 2, 3):
            s = add(zl, 4 - d, 4)
            recv(xg.at[k, core, x, s], aS.at[k, d - 1], aR.at[k, d - 1], {"zl": s})
        mine = xg.at[k, core, x]
        for d in (1, 2, 3):
            send(mine, mine, aS.at[k, d + 2], aR.at[k, d + 2], {"x": add(x, d, 4)})

    def a3(k):
        for d in (1, 2, 3):
            s = add(x, 4 - d, 4)
            recv(xg.at[k, core, s], aS.at[k, d + 2], aR.at[k, d + 2], {"x": s})
        mine = xg.at[k, core]
        send(mine, mine, aS.at[k, 6], aR.at[k, 6], {"core": 1 - core})

    def mm(j):
        k = j // 2
        half = core if own_half(j) else 1 - core
        if not own_half(j):
            recv(xg.at[k, half], aS.at[k, 6], aR.at[k, 6], {"core": 1 - core})
        if not weights:
            weights.append(True)
            w_copies[0].wait()
            w_copies[1].wait()

        def tile(n, carry):
            cols = pl.ds(pl.multiple_of(n * 256, 256), 256)
            r = jnp.dot(
                xg[k, half].reshape(C, xg.shape[-1]), wgu[:, cols], preferred_element_type=F32
            )
            part[j, :, :, cols] = r.astype(BF16).reshape(4, PR, 256)
            return carry

        lax.fori_loop(0, 2 * F // 256, tile, 0, unroll=True)
        send(part.at[j, y2, :, pl.ds(0, F)], r1.at[j, 0], bS.at[j, 0], bR.at[j, 0], {"y": yp})
        send(part.at[j, y2, :, pl.ds(F, F)], r1.at[j, 1], bS.at[j, 1], bR.at[j, 1], {"y": ym})

    def p2(j):
        recv(r1.at[j, 0], bS.at[j, 0], bR.at[j, 0], {"y": ym})
        a = part[j, yp, :, :F].astype(F32) + r1[j, 0].astype(F32)
        part[j, yp, :, :F] = a.astype(BF16)
        send(part.at[j, yp], r2.at[j, 0], bS.at[j, 2], bR.at[j, 2], {"y": yp})
        recv(r1.at[j, 1], bS.at[j, 1], bR.at[j, 1], {"y": yp})
        a = part[j, ym, :, F:].astype(F32) + r1[j, 1].astype(F32)
        part[j, ym, :, F:] = a.astype(BF16)
        send(part.at[j, ym], r2.at[j, 1], bS.at[j, 3], bR.at[j, 3], {"y": ym})

    def ysum(j, z, cols):
        rows = pl.ds(pl.multiple_of(z * ZR, ZR), ZR)
        s = part[j, y, rows, cols].astype(F32)
        return s + r2[j, 0, rows, cols].astype(F32) + r2[j, 1, rows, cols].astype(F32)

    def zsend(j):
        recv(r2.at[j, 0], bS.at[j, 2], bR.at[j, 2], {"y": ym})
        recv(r2.at[j, 1], bS.at[j, 3], bR.at[j, 3], {"y": yp})
        for cols in (slice(0, F), slice(F, 2 * F)):
            zs[j, :, cols] = ysum(j, 1 - zh, cols).astype(BF16)
        send(zs.at[j], zr.at[j], bS.at[j, 4], bR.at[j, 4], {"zh": 1 - zh})

    def hid(j):
        recv(zr.at[j], bS.at[j, 4], bR.at[j, 4], {"zh": 1 - zh})
        g = ysum(j, zh, slice(0, F)) + zr[j, :, :F].astype(F32)
        u = ysum(j, zh, slice(F, 2 * F)) + zr[j, :, F:].astype(F32)
        k = j // 2
        scale = sc[core if own_half(j) else 1 - core, k].reshape(ZR, 128)[:, 0:1]
        g = g * scale
        u = u * scale
        hg[j, y, zh] = (jax.nn.silu(g) * u).astype(BF16)
        mine = hg.at[j, y, zh]
        send(mine, mine, cS.at[j, 0], cR.at[j, 0], {"zh": 1 - zh})

    def cy(j):
        recv(hg.at[j, y, 1 - zh], cS.at[j, 0], cR.at[j, 0], {"zh": 1 - zh})
        mine = hg.at[j, y]
        send(mine, mine, cS.at[j, 1], cR.at[j, 1], {"y": yp})
        send(mine, mine, cS.at[j, 2], cR.at[j, 2], {"y": ym})

    def cf(j):
        recv(hg.at[j, ym], cS.at[j, 1], cR.at[j, 1], {"y": ym})
        send(hg.at[j, ym, 0], hg.at[j, ym, 0], cS.at[j, 3], cR.at[j, 3], {"y": yp})
        recv(hg.at[j, yp], cS.at[j, 2], cR.at[j, 2], {"y": yp})
        send(hg.at[j, yp, 1], hg.at[j, yp, 1], cS.at[j, 4], cR.at[j, 4], {"y": ym})

    def dn(j):
        k = j // 2
        recv(hg.at[j, y2, 0], cS.at[j, 3], cR.at[j, 3], {"y": ym})
        recv(hg.at[j, y2, 1], cS.at[j, 4], cR.at[j, 4], {"y": yp})
        if len(weights) == 1:
            weights.append(True)
            w_copies[2].wait()

        def tile(n, carry):
            cols = pl.ds(pl.multiple_of(n * 256, 256), 256)
            r = jnp.dot(hg[j].reshape(C, F), wd[:, cols], preferred_element_type=F32)
            r = r.reshape(4, 4 * R, 256)
            if own_half(j):
                oacc[k, :, :, cols] = r
            else:
                d1s[k, :, :, cols] = r.astype(BF16)
            return carry

        lax.fori_loop(0, wd.shape[1] // 256, tile, 0, unroll=True)
        if not own_half(j):
            send(d1s.at[k], d1r.at[k], dS.at[k, 0], dR.at[k, 0], {"core": 1 - core})

    def d2(k):
        recv(d1r.at[k], dS.at[k, 0], dR.at[k, 0], {"core": 1 - core})
        for i in range(4):
            s = oacc[k, i] + d1r[k, i].astype(F32)
            oacc[k, i] = s
            d2s[k, i] = s.astype(BF16)
        for d in (1, 2, 3):
            t = add(x, d, 4)
            send(d2s.at[k, t], d2r.at[k, d - 1], dS.at[k, d], dR.at[k, d], {"x": t})

    def d3(k):
        s = oacc[k, x]
        for d in (1, 2, 3):
            recv(d2r.at[k, d - 1], dS.at[k, d], dR.at[k, d], {"x": add(x, d, 4)})
            s = s + d2r[k, d - 1].astype(F32)
        s = s.reshape(4, R, s.shape[-1])
        o3[k] = s
        d3s[k] = s.astype(BF16)
        for d in (1, 2, 3):
            t = add(zl, d, 4)
            send(d3s.at[k, t], d3r.at[k, d - 1], dS.at[k, d + 3], dR.at[k, d + 3], {"zl": t})

    def d4(k):
        s = tok[k * R : (k + 1) * R, :].astype(F32) + o3[k, zl]
        for d in (1, 2, 3):
            recv(d3r.at[k, d - 1], dS.at[k, d + 3], dR.at[k, d + 3], {"zl": add(zl, d, 4)})
            s = s + d3r[k, d - 1].astype(F32)
        out[k * R : (k + 1) * R, :] = s.astype(BF16)

    weights = []
    ops = (a2, a3, mm, p2, zsend, hid, cy, cf, dn, d2, d3, d4, s1, s2, s3, s4)
    for o in ORDER:
        ops[o // 16](o % 16)
    for c in pending:
        c.wait_send()


def shards(tokens, norm_gain, gate_proj, up_proj, down_proj):
    T, DB = tokens.shape
    F = gate_proj.shape[1]
    R = T // K
    PR, ZR, H = 4 * R, 2 * R, 2 * K
    vmem = pl.BlockSpec(memory_space=pltpu.VMEM)
    hbm = pl.BlockSpec(memory_space=pl.ANY)
    dma = pltpu.SemaphoreType.DMA
    return pl.pallas_call(
        body,
        out_shape=jax.ShapeDtypeStruct((T, DB), BF16),
        in_specs=[hbm, hbm, hbm, hbm, hbm],
        out_specs=vmem,
        scratch_shapes=[
            pltpu.VMEM((T, DB), BF16),
            pltpu.VMEM((DB,), BF16),
            pltpu.VMEM((DB, 2 * F), BF16),
            pltpu.VMEM((F, DB), BF16),
            pltpu.VMEM((8, 8, 128), F32),
            pltpu.VMEM((2, 4, 4, 8, 128), F32),
            pltpu.VMEM((2, K, 2, R, 128), F32),
            pltpu.VMEM((K, 2, 4, 4, R, DB), BF16),
            pltpu.VMEM((H, 4, PR, 2 * F), BF16),
            pltpu.VMEM((H, 2, PR, F), BF16),
            pltpu.VMEM((H, 2, PR, 2 * F), BF16),
            pltpu.VMEM((H, ZR, 2 * F), BF16),
            pltpu.VMEM((H, ZR, 2 * F), BF16),
            pltpu.VMEM((H, 4, 2, ZR, F), BF16),
            pltpu.VMEM((K, 4, 4 * R, DB), F32),
            pltpu.VMEM((K, 4, 4 * R, DB), BF16),
            pltpu.VMEM((K, 4, 4 * R, DB), BF16),
            pltpu.VMEM((K, 4, 4 * R, DB), BF16),
            pltpu.VMEM((K, 3, 4 * R, DB), BF16),
            pltpu.VMEM((K, 4, R, DB), F32),
            pltpu.VMEM((K, 4, R, DB), BF16),
            pltpu.VMEM((K, 3, R, DB), BF16),
            dma((5,)),
            dma((8,)),
            dma((8,)),
            dma((7,)),
            dma((7,)),
            dma((K, 7)),
            dma((K, 7)),
            dma((H, 5)),
            dma((H, 5)),
            dma((H, 5)),
            dma((H, 5)),
            dma((K, 7)),
            dma((K, 7)),
        ],
        compiler_params=pltpu.CompilerParams(
            collective_id=0, has_side_effects=True, vmem_limit_bytes=60 * 2**20
        ),
        name="ffn",
    )(tokens, norm_gain, gate_proj, up_proj, down_proj)


def solution(mesh):
    split = Mesh(mesh.devices.reshape(4, 4, 2, 2, 4), ROW + COL)
    return jax.shard_map(
        shards,
        mesh=split,
        in_specs=(P(ROW, COL), P(COL), P(COL, ROW), P(COL, ROW), P(ROW, COL)),
        out_specs=P(ROW, COL),
        check_vma=False,
    )
```

time: 181 us -> 136 us (0.75)
  the two profiles are of different devices: /device:TPU:128 before, /device:TPU:8 now
where the time goes in v2:
time: 136 us; the launch traced here: 135 us
  Pallas kernels  133 us (98%)
  local copies, waits for them, and re-layouts  1.57 us (1%)
    pallas_call x1, Pallas kernels, shards(): pl.pallas_call(body, out_shape=jax.ShapeDtypeStruct((T, DB), BF16), in_sp...  133 us

profile of v2, /device:TPU:8, one launch (start us, length us, event | category | flops | bytes accessed | tf_op | source)
XLA Modules:
  0.0 134.8 jit_solution(5901378986029395522)
XLA Ops:
  0.0 133.2 %ffn.1 = bf16[64,1024]{1,0:T(8,128)(2,1)} custom-call(bf16[64,1024]{1,0:T(8,128)(2,1)} %tok_hbm.1, bf16[1024]{0:T(1024)(128)(2,1)} %gain_hbm.1, bf16[1024,896]{1,0:T(8,128)(2,1)} %gate.1, bf16[1024,896]{1,0:T(8,128)(2,1)} %up.1, bf16[896,1024]{1,0:T(8,128)(2,1)} %down.1), custom_call_target="tpu_custom_call" | custom-call | tf_op jit(solution)/shard_map/ffn/pallas_call | solution.py:300
  133.2 1.6 %copy.7 = bf16[64,1024]{1,0:T(8,128)(2,1)} copy(bf16[64,1024]{1,0:T(8,128)(2,1)} %ffn.1) | data formatting | bytes 262144

commit v3 on v2

--- a/solution.py
+++ b/solution.py
@@ -12,36 +12,38 @@
 ROW = ("zl", "x", "core")
 COL = ("zh", "y")
 
-K = 8
+G = 2
+DX = ((0, 1, 3, 2), (2, 3, 1, 0))
 F32 = jnp.float32
 BF16 = jnp.bfloat16
 
-STEPS = ("a2", "a3", "mm", "p2", "zs", "hid", "cy", "cf", "dn", "d2", "d3", "d4", "s1", "s2", "s3", "s4")
+STEPS = (
+    "a1", "a2", "a3", "mm", "p2", "zs", "hid", "cy", "cf", "dn", "d2", "d3", "d4", "s1", "s2", "s3", "s4",
+)
 ORDER = (
-    0, 1, 4, 16, 2, 32, 33, 17, 34, 48, 3, 192, 6, 20, 49, 18, 35, 208, 50, 37,
-    41, 64, 7, 5, 19, 224, 40, 65, 36, 53, 240, 80, 57, 23, 21, 66, 43, 38, 52, 69,
-    81, 51, 42, 82, 56, 54, 59, 67, 73, 68, 97, 39, 85, 58, 72, 83, 22, 44, 113, 84,
-    55, 75, 45, 70, 60, 71, 129, 61, 96, 101, 74, 98, 47, 100, 89, 91, 112, 88, 76, 99,
-    87, 90, 86, 46, 63, 77, 128, 62, 117, 114, 116, 103, 79, 115, 78, 133, 102, 130, 105, 104,
-    144, 106, 132, 93, 119, 146, 92, 95, 131, 121, 118, 94, 145, 107, 120, 108, 135, 134, 162, 122,
-    109, 147, 136, 123, 110, 137, 148, 124, 125, 111, 138, 139, 149, 126, 140, 127, 141, 150, 163, 164,
-    160, 142, 143, 151, 179, 165, 161, 166, 176, 167, 177, 181, 182, 180, 178, 183,
+    1, 16, 48, 49, 64, 33, 34, 65, 208, 52, 17, 53, 51, 68, 35, 50, 55, 67, 69, 81,
+    54, 84, 37, 71, 224, 38, 36, 83, 66, 57, 80, 58, 87, 59, 70, 85, 82, 240, 62, 74,
+    256, 97, 103, 56, 75, 86, 100, 98, 60, 61, 99, 72, 90, 63, 102, 76, 119, 77, 91, 78,
+    101, 79, 106, 92, 107, 93, 115, 73, 88, 94, 122, 114, 108, 131, 89, 123, 118, 104, 96, 109,
+    135, 130, 139, 116, 147, 138, 134, 95, 117, 151, 132, 105, 146, 113, 161, 124, 133, 150, 163, 148,
+    110, 125, 155, 154, 111, 120, 140, 149, 165, 121, 162, 141, 136, 126, 156, 137, 112, 129, 157, 152,
+    166, 127, 153, 128, 164, 142, 145, 143, 144, 160, 176, 158, 159, 167, 177, 192, 193,
 )
 
 
 def own_half(j):
-    return (j % 2 == 0) == (j // 2 < K // 2)
+    return (j % 2 == 0) == (j < 8)
 
 
 def body(
     tok_hbm, gain_hbm, gate, up, down, out,
     tok, gain, wgu, wd, sq, sg, sc, xg, part, r1, r2, zs, zr, hg, oacc, d1s, d1r, d2s, d2r, o3, d3s, d3r,
-    wsem, sqS, sqR, eS, eR, aS, aR, bS, bR, cS, cR, dS, dR,
+    wsem, sqS, sqR, eS, eR, aS, aR, bS, bR, cS, cR, dS, dR, fS, fR,
 ):
     zl, x, core, zh, y = [lax.axis_index(n) for n in ("zl", "x", "core", "zh", "y")]
     F = gate.shape[1]
-    R = tok.shape[0] // K
-    PR, ZR, C = 4 * R, 2 * R, 16 * R
+    Q = tok.shape[0] // G
+    PR, ZR, C = Q, Q // 2, 4 * Q
     col = zh * 4 + y
 
     def add(v, d, n):
@@ -96,22 +98,27 @@
         v = tok[:, cols].astype(F32)
         acc = acc + v * v
         v = (v * gain_row[:, cols]).astype(BF16)
-        for k in range(K):
-            xg[k, core, x, zl, :, cols] = v[k * R : (k + 1) * R]
+        for g2 in range(G):
+            xg[g2, x, core, zl, :, cols] = v[g2 * Q : (g2 + 1) * Q]
     acc = jnp.concatenate([acc, jnp.zeros((128 - tok.shape[0], 128), F32)], axis=0)
     sq[col] = jnp.broadcast_to(jnp.sum(acc.T, axis=0, keepdims=True), (8, 128))
     pl.semaphore_wait(barrier, len(peers))
 
-    def a1(k):
-        mine = xg.at[k, core, x, zl]
-        for d in (1, 2, 3):
-            send(mine, mine, aS.at[k, d - 1], aR.at[k, d - 1], {"zl": add(zl, d, 4)})
+    def xsend(g, d, b):
+        mine = xg.at[g, x, core, add(zl, b, 4)]
+        i = 3 + 4 * (d - 1) + b
+        send(mine, mine, aS.at[g, i], aR.at[g, i], {"x": add(x, d, 4)})
+
+    def a1(g):
+        mine = xg.at[g, x, core, zl]
+        for d in (1, 2, 3):
+            send(mine, mine, aS.at[g, d - 1], aR.at[g, d - 1], {"zl": add(zl, d, 4)})
+        for d in (1, 3, 2):
+            xsend(g, d, 0)
 
     a1(0)
     for d in range(1, 8):
         send(sq.at[col], sq.at[col], sqS.at[d], sqR.at[d], colpeer(d))
-    for k in range(1, K):
-        a1(k)
 
     def s1(_):
         for d in range(1, 8):
@@ -143,30 +150,35 @@
     def s4(_):
         recv(sg.at[1 - core], eS.at[6], eR.at[6], {"core": 1 - core})
         for h in (0, 1):
-            for i in (0, 1):
-                v = jnp.broadcast_to(sg[h, y, 2 * zh + i][0:1, :], (128, 128)).T
-                sc[h, :, i] = v[: K * R, :].reshape(K, R, 128)
-
-    def a2(k):
-        for d in (1, 2, 3):
-            s = add(zl, 4 - d, 4)
-            recv(xg.at[k, core, x, s], aS.at[k, d - 1], aR.at[k, d - 1], {"zl": s})
-        mine = xg.at[k, core, x]
-        for d in (1, 2, 3):
-            send(mine, mine, aS.at[k, d + 2], aR.at[k, d + 2], {"x": add(x, d, 4)})
-
-    def a3(k):
-        for d in (1, 2, 3):
-            s = add(x, 4 - d, 4)
-            recv(xg.at[k, core, s], aS.at[k, d + 2], aR.at[k, d + 2], {"x": s})
-        mine = xg.at[k, core]
-        send(mine, mine, aS.at[k, 6], aR.at[k, 6], {"core": 1 - core})
+            for dx in range(4):
+                v = jnp.broadcast_to(sg[h, add(x, dx, 4), y][0:1, :], (128, 128)).T
+                sc[h, dx] = v[: G * Q, :].reshape(G, 2, ZR, 128)
+
+    def a2(g):
+        for d in (1, 2, 3):
+            t = add(zl, 4 - d, 4)
+            recv(xg.at[g, x, core, t], aS.at[g, d - 1], aR.at[g, d - 1], {"zl": t})
+        mine = xg.at[g, x, core]
+        send(mine, mine, aS.at[g, 15], aR.at[g, 15], {"core": 1 - core})
+        for b in (1, 2, 3):
+            for d in (1, 3, 2):
+                xsend(g, d, b)
+
+    def a3(c):
+        g, dx = c // 4, DX[c // 4][c % 4]
+        src, d = add(x, dx, 4), 4 - dx
+        for b in range(4):
+            i = 3 + 4 * (d - 1) + b
+            recv(xg.at[g, src, core, add(zl, b, 4)], aS.at[g, i], aR.at[g, i], {"x": src})
+        mine = xg.at[g, src, core]
+        send(mine, mine, aS.at[g, 15 + dx], aR.at[g, 15 + dx], {"core": 1 - core})
 
     def mm(j):
-        k = j // 2
+        g, dx = j // 8, DX[j // 8][j // 2 % 4]
+        src = add(x, dx, 4)
         half = core if own_half(j) else 1 - core
         if not own_half(j):
-            recv(xg.at[k, half], aS.at[k, 6], aR.at[k, 6], {"core": 1 - core})
+            recv(xg.at[g, src, half], aS.at[g, 15 + dx], aR.at[g, 15 + dx], {"core": 1 - core})
         if not weights:
             weights.append(True)
             w_copies[0].wait()
@@ -175,7 +187,7 @@
         def tile(n, carry):
             cols = pl.ds(pl.multiple_of(n * 256, 256), 256)
             r = jnp.dot(
-                xg[k, half].reshape(C, xg.shape[-1]), wgu[:, cols], preferred_element_type=F32
+                xg[g, src, half].reshape(C, xg.shape[-1]), wgu[:, cols], preferred_element_type=F32
             )
             part[j, :, :, cols] = r.astype(BF16).reshape(4, PR, 256)
             return carry
@@ -210,8 +222,8 @@
         recv(zr.at[j], bS.at[j, 4], bR.at[j, 4], {"zh": 1 - zh})
         g = ysum(j, zh, slice(0, F)) + zr[j, :, :F].astype(F32)
         u = ysum(j, zh, slice(F, 2 * F)) + zr[j, :, F:].astype(F32)
-        k = j // 2
-        scale = sc[core if own_half(j) else 1 - core, k].reshape(ZR, 128)[:, 0:1]
+        g2, dx = j // 8, DX[j // 8][j // 2 % 4]
+        scale = sc[core if own_half(j) else 1 - core, dx, g2, zh][:, 0:1]
         g = g * scale
         u = u * scale
         hg[j, y, zh] = (jax.nn.silu(g) * u).astype(BF16)
@@ -241,7 +253,7 @@
         def tile(n, carry):
             cols = pl.ds(pl.multiple_of(n * 256, 256), 256)
             r = jnp.dot(hg[j].reshape(C, F), wd[:, cols], preferred_element_type=F32)
-            r = r.reshape(4, 4 * R, 256)
+            r = r.reshape(4, Q, 256)
             if own_half(j):
                 oacc[k, :, :, cols] = r
             else:
@@ -252,37 +264,42 @@
         if not own_half(j):
             send(d1s.at[k], d1r.at[k], dS.at[k, 0], dR.at[k, 0], {"core": 1 - core})
 
-    def d2(k):
-        recv(d1r.at[k], dS.at[k, 0], dR.at[k, 0], {"core": 1 - core})
+    def d2(c):
+        dx = DX[c // 4][c % 4]
+        recv(d1r.at[c], dS.at[c, 0], dR.at[c, 0], {"core": 1 - core})
         for i in range(4):
-            s = oacc[k, i] + d1r[k, i].astype(F32)
-            oacc[k, i] = s
-            d2s[k, i] = s.astype(BF16)
-        for d in (1, 2, 3):
-            t = add(x, d, 4)
-            send(d2s.at[k, t], d2r.at[k, d - 1], dS.at[k, d], dR.at[k, d], {"x": t})
-
-    def d3(k):
-        s = oacc[k, x]
-        for d in (1, 2, 3):
-            recv(d2r.at[k, d - 1], dS.at[k, d], dR.at[k, d], {"x": add(x, d, 4)})
-            s = s + d2r[k, d - 1].astype(F32)
-        s = s.reshape(4, R, s.shape[-1])
-        o3[k] = s
-        d3s[k] = s.astype(BF16)
+            s = oacc[c, i] + d1r[c, i].astype(F32)
+            if dx:
+                d2s[c, i] = s.astype(BF16)
+            else:
+                oacc[c, i] = s
+        if dx:
+            send(d2s.at[c], d2r.at[c], dS.at[c, 1], dR.at[c, 1], {"x": add(x, dx, 4)})
+
+    def d3(g):
+        mine = 4 * g + DX[g].index(0)
+        others = [4 * g + i for i in range(4) if DX[g][i]]
+        for c in others:
+            recv(d2r.at[c], dS.at[c, 1], dR.at[c, 1], {"x": add(x, 1, 4)})
+        for i in range(4):
+            s = oacc[mine, i]
+            for c in others:
+                s = s + d2r[c, i].astype(F32)
+            o3[g, i] = s
+            d3s[g, i] = s.astype(BF16)
         for d in (1, 2, 3):
             t = add(zl, d, 4)
-            send(d3s.at[k, t], d3r.at[k, d - 1], dS.at[k, d + 3], dR.at[k, d + 3], {"zl": t})
-
-    def d4(k):
-        s = tok[k * R : (k + 1) * R, :].astype(F32) + o3[k, zl]
-        for d in (1, 2, 3):
-            recv(d3r.at[k, d - 1], dS.at[k, d + 3], dR.at[k, d + 3], {"zl": add(zl, d, 4)})
-            s = s + d3r[k, d - 1].astype(F32)
-        out[k * R : (k + 1) * R, :] = s.astype(BF16)
+            send(d3s.at[g, t], d3r.at[g, d - 1], fS.at[g, d - 1], fR.at[g, d - 1], {"zl": t})
+
+    def d4(g):
+        s = tok[g * Q : (g + 1) * Q, :].astype(F32) + o3[g, zl]
+        for d in (1, 2, 3):
+            recv(d3r.at[g, d - 1], fS.at[g, d - 1], fR.at[g, d - 1], {"zl": add(zl, d, 4)})
+            s = s + d3r[g, d - 1].astype(F32)
+        out[g * Q : (g + 1) * Q, :] = s.astype(BF16)
 
     weights = []
-    ops = (a2, a3, mm, p2, zsend, hid, cy, cf, dn, d2, d3, d4, s1, s2, s3, s4)
+    ops = (a1, a2, a3, mm, p2, zsend, hid, cy, cf, dn, d2, d3, d4, s1, s2, s3, s4)
     for o in ORDER:
         ops[o // 16](o % 16)
     for c in pending:
@@ -292,8 +309,8 @@
 def shards(tokens, norm_gain, gate_proj, up_proj, down_proj):
     T, DB = tokens.shape
     F = gate_proj.shape[1]
-    R = T // K
-    PR, ZR, H = 4 * R, 2 * R, 2 * K
+    Q = T // G
+    PR, ZR, H, N = Q, Q // 2, 16, 8
     vmem = pl.BlockSpec(memory_space=pltpu.VMEM)
     hbm = pl.BlockSpec(memory_space=pl.ANY)
     dma = pltpu.SemaphoreType.DMA
@@ -309,35 +326,37 @@
             pltpu.VMEM((F, DB), BF16),
             pltpu.VMEM((8, 8, 128), F32),
             pltpu.VMEM((2, 4, 4, 8, 128), F32),
-            pltpu.VMEM((2, K, 2, R, 128), F32),
-            pltpu.VMEM((K, 2, 4, 4, R, DB), BF16),
+            pltpu.VMEM((2, 4, G, 2, ZR, 128), F32),
+            pltpu.VMEM((G, 4, 2, 4, Q, DB), BF16),
             pltpu.VMEM((H, 4, PR, 2 * F), BF16),
             pltpu.VMEM((H, 2, PR, F), BF16),
             pltpu.VMEM((H, 2, PR, 2 * F), BF16),
             pltpu.VMEM((H, ZR, 2 * F), BF16),
             pltpu.VMEM((H, ZR, 2 * F), BF16),
             pltpu.VMEM((H, 4, 2, ZR, F), BF16),
-            pltpu.VMEM((K, 4, 4 * R, DB), F32),
-            pltpu.VMEM((K, 4, 4 * R, DB), BF16),
-            pltpu.VMEM((K, 4, 4 * R, DB), BF16),
-            pltpu.VMEM((K, 4, 4 * R, DB), BF16),
-            pltpu.VMEM((K, 3, 4 * R, DB), BF16),
-            pltpu.VMEM((K, 4, R, DB), F32),
-            pltpu.VMEM((K, 4, R, DB), BF16),
-            pltpu.VMEM((K, 3, R, DB), BF16),
+            pltpu.VMEM((N, 4, Q, DB), F32),
+            pltpu.VMEM((N, 4, Q, DB), BF16),
+            pltpu.VMEM((N, 4, Q, DB), BF16),
+            pltpu.VMEM((N, 4, Q, DB), BF16),
+            pltpu.VMEM((N, 4, Q, DB), BF16),
+            pltpu.VMEM((G, 4, Q, DB), F32),
+            pltpu.VMEM((G, 4, Q, DB), BF16),
+            pltpu.VMEM((G, 3, Q, DB), BF16),
             dma((5,)),
             dma((8,)),
             dma((8,)),
             dma((7,)),
             dma((7,)),
-            dma((K, 7)),
-            dma((K, 7)),
+            dma((G, 19)),
+            dma((G, 19)),
             dma((H, 5)),
             dma((H, 5)),
             dma((H, 5)),
             dma((H, 5)),
-            dma((K, 7)),
-            dma((K, 7)),
+            dma((N, 2)),
+            dma((N, 2)),
+            dma((G, 3)),
+            dma((G, 3)),
         ],
         compiler_params=pltpu.CompilerParams(
             collective_id=0, has_side_effects=True, vmem_limit_bytes=60 * 2**20

time: 136 us -> 136 us (level)
  no operation moved by 1% of the time
where the time goes in v3:
time: 136 us; the launch traced here: 135 us
  Pallas kernels  133 us (98%)
  local copies, waits for them, and re-layouts  1.57 us (1%)
    pallas_call x1, Pallas kernels, shards(): pl.pallas_call(body, out_shape=jax.ShapeDtypeStruct((T, DB), BF16), in_sp...  133 us

profile of v3, /device:TPU:8, one launch (start us, length us, event | category | flops | bytes accessed | tf_op | source)
XLA Modules:
  0.0 135.0 jit_solution(14417973055874612632)
XLA Ops:
  0.0 133.5 %ffn.1 = bf16[64,1024]{1,0:T(8,128)(2,1)} custom-call(bf16[64,1024]{1,0:T(8,128)(2,1)} %tok_hbm.1, bf16[1024]{0:T(1024)(128)(2,1)} %gain_hbm.1, bf16[1024,896]{1,0:T(8,128)(2,1)} %gate.1, bf16[1024,896]{1,0:T(8,128)(2,1)} %up.1, bf16[896,1024]{1,0:T(8,128)(2,1)} %down.1), custom_call_target="tpu_custom_call" | custom-call | tf_op jit(solution)/shard_map/ffn/pallas_call | solution.py:317
  133.5 1.6 %copy.7 = bf16[64,1024]{1,0:T(8,128)(2,1)} copy(bf16[64,1024]{1,0:T(8,128)(2,1)} %ffn.1) | data formatting | bytes 262144

commit v4 on v3

--- a/solution.py
+++ b/solution.py
@@ -21,13 +21,13 @@
     "a1", "a2", "a3", "mm", "p2", "zs", "hid", "cy", "cf", "dn", "d2", "d3", "d4", "s1", "s2", "s3", "s4",
 )
 ORDER = (
-    1, 16, 48, 49, 64, 33, 34, 65, 208, 52, 17, 53, 51, 68, 35, 50, 55, 67, 69, 81,
-    54, 84, 37, 71, 224, 38, 36, 83, 66, 57, 80, 58, 87, 59, 70, 85, 82, 240, 62, 74,
-    256, 97, 103, 56, 75, 86, 100, 98, 60, 61, 99, 72, 90, 63, 102, 76, 119, 77, 91, 78,
-    101, 79, 106, 92, 107, 93, 115, 73, 88, 94, 122, 114, 108, 131, 89, 123, 118, 104, 96, 109,
-    135, 130, 139, 116, 147, 138, 134, 95, 117, 151, 132, 105, 146, 113, 161, 124, 133, 150, 163, 148,
-    110, 125, 155, 154, 111, 120, 140, 149, 165, 121, 162, 141, 136, 126, 156, 137, 112, 129, 157, 152,
-    166, 127, 153, 128, 164, 142, 145, 143, 144, 160, 176, 158, 159, 167, 177, 192, 193,
+    1, 16, 48, 49, 208, 64, 33, 34, 65, 224, 51, 52, 53, 80, 50, 17, 240, 67, 81, 35,
+    69, 68, 256, 96, 54, 83, 37, 85, 55, 38, 66, 60, 61, 70, 84, 97, 36, 57, 82, 71,
+    58, 101, 77, 76, 59, 86, 100, 98, 56, 62, 87, 99, 74, 93, 92, 117, 75, 116, 103, 90,
+    102, 63, 114, 109, 72, 91, 73, 133, 79, 119, 108, 78, 88, 89, 118, 130, 149, 115, 106, 107,
+    95, 124, 132, 134, 135, 125, 112, 94, 104, 131, 148, 140, 105, 162, 122, 150, 113, 151, 146, 163,
+    123, 147, 141, 111, 110, 156, 138, 120, 161, 121, 157, 139, 166, 129, 154, 136, 137, 128, 126, 155,
+    165, 127, 145, 152, 153, 164, 144, 142, 160, 176, 143, 158, 159, 167, 177, 192, 193,
 )
 
 

time: 136 us -> 137 us (level)
  no operation moved by 1% of the time
where the time goes in v4:
time: 137 us; the launch traced here: 135 us
  Pallas kernels  134 us (98%)
  local copies, waits for them, and re-layouts  1.57 us (1%)
    pallas_call x1, Pallas kernels, shards(): pl.pallas_call(body, out_shape=jax.ShapeDtypeStruct((T, DB), BF16), in_sp...  134 us

profile of v4, /device:TPU:8, one launch (start us, length us, event | category | flops | bytes accessed | tf_op | source)
XLA Modules:
  0.0 135.3 jit_solution(11246921922122009628)
XLA Ops:
  0.0 133.8 %ffn.1 = bf16[64,1024]{1,0:T(8,128)(2,1)} custom-call(bf16[64,1024]{1,0:T(8,128)(2,1)} %tok_hbm.1, bf16[1024]{0:T(1024)(128)(2,1)} %gain_hbm.1, bf16[1024,896]{1,0:T(8,128)(2,1)} %gate.1, bf16[1024,896]{1,0:T(8,128)(2,1)} %up.1, bf16[896,1024]{1,0:T(8,128)(2,1)} %down.1), custom_call_target="tpu_custom_call" | custom-call | tf_op jit(solution)/shard_map/ffn/pallas_call | solution.py:317
  133.8 1.6 %copy.7 = bf16[64,1024]{1,0:T(8,128)(2,1)} copy(bf16[64,1024]{1,0:T(8,128)(2,1)} %ffn.1) | data formatting | bytes 262144

commit v5 on v2

--- a/solution.py
+++ b/solution.py
@@ -18,14 +18,14 @@
 
 STEPS = ("a2", "a3", "mm", "p2", "zs", "hid", "cy", "cf", "dn", "d2", "d3", "d4", "s1", "s2", "s3", "s4")
 ORDER = (
-    0, 1, 4, 16, 2, 32, 33, 17, 34, 48, 3, 192, 6, 20, 49, 18, 35, 208, 50, 37,
-    41, 64, 7, 5, 19, 224, 40, 65, 36, 53, 240, 80, 57, 23, 21, 66, 43, 38, 52, 69,
-    81, 51, 42, 82, 56, 54, 59, 67, 73, 68, 97, 39, 85, 58, 72, 83, 22, 44, 113, 84,
-    55, 75, 45, 70, 60, 71, 129, 61, 96, 101, 74, 98, 47, 100, 89, 91, 112, 88, 76, 99,
-    87, 90, 86, 46, 63, 77, 128, 62, 117, 114, 116, 103, 79, 115, 78, 133, 102, 130, 105, 104,
-    144, 106, 132, 93, 119, 146, 92, 95, 131, 121, 118, 94, 145, 107, 120, 108, 135, 134, 162, 122,
-    109, 147, 136, 123, 110, 137, 148, 124, 125, 111, 138, 139, 149, 126, 140, 127, 141, 150, 163, 164,
-    160, 142, 143, 151, 179, 165, 161, 166, 176, 167, 177, 181, 182, 180, 178, 183,
+    0, 1, 2, 192, 16, 32, 33, 17, 34, 5, 48, 4, 18, 49, 37, 21, 43, 50, 64, 208,
+    20, 53, 6, 36, 41, 224, 7, 65, 35, 59, 42, 66, 40, 69, 240, 80, 22, 51, 52, 75,
+    81, 56, 57, 82, 67, 3, 58, 68, 85, 23, 47, 46, 19, 73, 39, 91, 44, 72, 38, 96,
+    45, 55, 84, 62, 89, 97, 112, 83, 54, 74, 61, 60, 88, 71, 78, 70, 113, 90, 100, 87,
+    104, 76, 101, 129, 63, 128, 105, 86, 99, 120, 77, 103, 121, 117, 98, 79, 144, 116, 115, 136,
+    106, 102, 94, 119, 92, 137, 148, 93, 132, 114, 133, 107, 146, 122, 131, 95, 118, 110, 130, 145,
+    108, 123, 135, 109, 134, 126, 147, 124, 138, 111, 164, 162, 139, 125, 149, 160, 140, 142, 161, 127,
+    141, 150, 180, 178, 143, 163, 151, 166, 177, 179, 165, 167, 181, 176, 182, 183,
 )
 
 

time: 136 us -> 133 us (0.978)
  Pallas kernels: 133 us -> 131 us
    pallas_call x1, Pallas kernels: 133 us -> 131 us  [shards(): pl.pallas_call(body, out_shape=jax.ShapeDtypeStruct((T, DB), BF16), in_sp...]
where the time goes in v5:
time: 133 us; the launch traced here: 132 us
  Pallas kernels  131 us (98%)
  local copies, waits for them, and re-layouts  1.57 us (1%)
    pallas_call x1, Pallas kernels, shards(): pl.pallas_call(body, out_shape=jax.ShapeDtypeStruct((T, DB), BF16), in_sp...  131 us

profile of v5, /device:TPU:8, one launch (start us, length us, event | category | flops | bytes accessed | tf_op | source)
XLA Modules:
  0.0 132.4 jit_solution(13427948935511234281)
XLA Ops:
  0.0 130.9 %ffn.1 = bf16[64,1024]{1,0:T(8,128)(2,1)} custom-call(bf16[64,1024]{1,0:T(8,128)(2,1)} %tok_hbm.1, bf16[1024]{0:T(1024)(128)(2,1)} %gain_hbm.1, bf16[1024,896]{1,0:T(8,128)(2,1)} %gate.1, bf16[1024,896]{1,0:T(8,128)(2,1)} %up.1, bf16[896,1024]{1,0:T(8,128)(2,1)} %down.1), custom_call_target="tpu_custom_call" | custom-call | tf_op jit(solution)/shard_map/ffn/pallas_call | solution.py:300
  130.9 1.6 %copy.7 = bf16[64,1024]{1,0:T(8,128)(2,1)} copy(bf16[64,1024]{1,0:T(8,128)(2,1)} %ffn.1) | data formatting | bytes 262144
